TPU v7x, 32 devices: a whole 2x2x4 slice. The times are simulated.
32 devices in a mesh: row: 4 (over y, x), col: 8 (over z, core).
Axes of the slice: x: 2, y: 2, z: 4, core: 2. Of those that a mesh axis runs over, the one named last changes fastest.
Arguments:
- view_one: bfloat16 [2048, 8192], P('row', 'col'), may hold values from -6 to 6
- view_two: bfloat16 [2048, 8192], P('row', 'col'), may hold values from -6 to 6
- pair_weights: bfloat16 [8192, 8192], P('row', 'col'), may hold values from 0.25 to 2.5
Outputs:
- first_grad: bfloat16 [2048, 8192], P('row', 'col')
- second_grad: bfloat16 [2048, 8192], P('row', 'col')
All inputs are finite; a program needn't handle non-finite values.
Results may differ from a plain program's by a relative error of at most 0.004.
Values may be sent and summed in bfloat16 or wider, within the bound.
A program may use at most 128 MiB of HBM per device.

v0:
```python
import jax
import jax.numpy as jnp
from jax import lax
from jax.sharding import PartitionSpec as P


def per_device(view_one, view_two, pair_weights):
    wide_two = lax.all_gather(view_two, "col", axis=1, tiled=True)
    samples = view_one.shape[0] * lax.axis_size("row")
    local_rows = pair_weights.shape[0]
    local_cols = pair_weights.shape[1]
    regrouped = lax.all_to_all(wide_two, "row", split_axis=1, concat_axis=0, tiled=True)
    summed = lax.dot_general(
        regrouped,
        lax.all_gather(view_one, "row", axis=0, tiled=True),
        (((0,), (0,)), ((), ())),
        preferred_element_type=jnp.float32,
    )
    correlation = summed / samples
    row_ids = lax.axis_index("row") * local_rows + lax.broadcasted_iota(
        jnp.int32, (local_rows, local_cols), 0
    )
    col_ids = lax.axis_index("col") * local_cols + lax.broadcasted_iota(
        jnp.int32, (local_rows, local_cols), 1
    )
    identity = jnp.where(row_ids == col_ids, 1.0, 0.0).astype(jnp.float32)
    weighted = (pair_weights.astype(jnp.float32) * (correlation - identity)).astype(jnp.bfloat16)
    grad_cols = lax.all_gather(weighted, "row", axis=0, tiled=True)
    first_grad = jnp.dot(wide_two, grad_cols, preferred_element_type=jnp.float32).astype(
        jnp.bfloat16
    )
    second_flipped = lax.psum_scatter(
        lax.dot_general(
            grad_cols, view_one, (((1,), (1,)), ((), ())), preferred_element_type=jnp.float32
        ),
        "col",
        scatter_dimension=0,
        tiled=True,
    )
    return (first_grad, second_flipped.T.astype(jnp.bfloat16))


def solution(mesh):
    placed = (P("row", "col"), P("row", "col"), P("row", "col"))
    return jax.shard_map(
        per_device,
        mesh=mesh,
        in_specs=placed,
        out_specs=(P("row", "col"), P("row", "col")),
        check_vma=False,
    )
```

profile of v0, /device:TPU:0, one launch (start us, length us, event | category | flops | bytes accessed | tf_op | source)
XLA Modules:
  0.0 604.9 jit_solution(17463055193101031785)
XLA Ops:
  8.0 0.0 all-gather.4.cloned.1.call-start
  8.0 2.3 copy.9
  10.3 0.0 all-gather.4.cloned.1.call-update
  10.3 85.4 %all-gather.4.cloned.1.call-done = bf16[512,8192]{0,1:T(8,128)(2,1)} async-done(((bf16[512,1024]{0,1:T(8,128)(2,1)}), bf16[512,8192]{0,1:T(8,128)(2,1)}) %all-gather.4.cloned.1.call-update) | async-done | bytes 8388624 | tf_op jit(solution)/shard_map/all_gather | solution.py:8
  95.8 5.7 all-to-all-start
  101.4 0.0 all-gather.6.cloned.1.call-start
  101.5 0.5 all-gather.6.cloned.1.call-update
  102.0 0.0 all-gather.8.cloned.1.call-start
  102.1 126.1 %all-to-all-done = bf16[512,4,2048]{0,2,1:T(8,128)(2,1)} async-done(((bf16[512,4,2048]{0,2,1:T(8,128)(2,1)}), bf16[512,4,2048]{0,2,1:T(8,128)(2,1)}, u32[]{:S(2)}, u32[]{:S(2)}) %all-to-all-start) | async-done | bytes 8388640 | tf_op jit(solution)/shard_map/all_to_all | solution.py:12
  228.2 11.4 %copy.10 = bf16[4,512,2048]{2,1,0:T(8,128)(2,1)} copy(bf16[4,512,2048]{1,2,0:T(8,128)(2,1)} %bitcast.1) | data formatting | bytes 16777216 | tf_op jit(solution)/shard_map/all_to_all | solution.py:12
  239.6 0.0 all-gather.6.cloned.1.call-done
  239.6 0.0 copy-start
  239.6 15.8 %multiply_convert_fusion = bf16[2048,1024]{1,0:T(8,128)(2,1)} fusion(bf16[2048,1024]{1,0:T(8,128)(2,1)} %param.5, bf16[2048,2048]{1,0:T(8,128)(2,1)} %bitcast.14, bf16[2048,1024]{1,0:T(8,128)(2,1)} %all-gather.6.cloned.1.call-done, s32[1024]{0:T(1024)S(1)} %iota_add_fusion.1, s32[2048]{0:T(1024)S(1)} %iota_add_fusion), kind=kOutput, calls=%fused_computation | convolution fusion | flops 8604614656 | bytes 20983808 | tf_op jit(solution)/shard_map/dot_general | solution.py:13
  255.4 0.0 all-gather.8.cloned.1.call-update
  255.4 0.2 reduce-scatter.2.cloned.1.call-start
  255.7 154.6 %all-gather.8.cloned.1.call-done = bf16[8192,1024]{1,0:T(8,128)(2,1)} async-done(((bf16[2048,1024]{1,0:T(8,128)(2,1)}), bf16[8192,1024]{1,0:T(8,128)(2,1)}) %all-gather.8.cloned.1.call-update) | async-done | bytes 16777232 | tf_op jit(solution)/shard_map/all_gather | solution.py:28
  410.3 0.0 copy-done
  410.3 15.8 %fusion.1 = f32[8192,512]{1,0:T(8,128)} fusion(bf16[8192,1024]{1,0:T(8,128)(2,1)} %all-gather.8.cloned.1.call-done, bf16[512,1024]{1,0:T(8,128)(2,1)S(1)} %copy-done), kind=kOutput, calls=%fused_computation.6 | convolution fusion | flops 8589934592 | bytes 34603008 | tf_op jit(solution)/shard_map/dot_general | solution.py:33
  426.0 0.0 reduce-scatter.2.cloned.1.call-update
  426.1 14.8 %fusion = bf16[512,1024]{0,1:T(8,128)(2,1)S(1)} fusion(bf16[8192,1024]{1,0:T(8,128)(2,1)} %all-gather.8.cloned.1.call-done, bf16[512,8192]{0,1:T(8,128)(2,1)} %all-gather.4.cloned.1.call-done), kind=kOutput, calls=%fused_computation.2 | convolution fusion | flops 8590458880 | bytes 26214400 | tf_op jit(solution)/shard_map/dot_general | solution.py:29
  440.9 1.3 copy.11
  442.2 152.2 %reduce-scatter.2.cloned.1.call-done = f32[1024,512]{1,0:T(8,128)} async-done(((f32[8192,512]{1,0:T(8,128)}), f32[1024,512]{1,0:T(8,128)}) %reduce-scatter.2.cloned.1.call-update) | async-done | bytes 2097168 | tf_op jit(solution)/shard_map/reduce_scatter | solution.py:32
  594.4 1.7 convert_bitcast_fusion
  596.1 1.3 copy.12
  (2 shorter events, 0.0 us)
Async XLA Ops:
  8.0 87.8 %all-gather.4.cloned.1.call-start = ((), (), s32[]{:S(2)}) async-start(), calls=%async_computation.2 | async-start | bytes 9437184 | tf_op jit(solution)/shard_map/all_gather | solution.py:8
  95.8 132.4 %all-to-all-start = ((bf16[512,4,2048]{0,2,1:T(8,128)(2,1)}), bf16[512,4,2048]{0,2,1:T(8,128)(2,1)}, u32[]{:S(2)}, u32[]{:S(2)}) async-start(bf16[512,4,2048]{0,2,1:T(8,128)(2,1)} %bitcast.13), calls=%async_computation | async-start | bytes 16777216 | tf_op jit(solution)/shard_map/all_to_all | solution.py:12
  101.4 138.2 %all-gather.6.cloned.1.call-start = ((), (), s32[]{:S(2)}) async-start(), calls=%async_computation.3 | async-start | bytes 5242880 | tf_op jit(solution)/shard_map/all_gather | solution.py:15
  102.0 308.3 %all-gather.8.cloned.1.call-start = ((), (), s32[]{:S(2)}) async-start(), calls=%async_computation.4 | async-start | bytes 20971520 | tf_op jit(solution)/shard_map/all_gather | solution.py:28
  239.6 170.7 %copy-start = (bf16[512,1024]{1,0:T(8,128)(2,1)S(1)}, bf16[512,1024]{1,0:T(8,128)(2,1)}, u32[]{:S(2)}) copy-start(bf16[512,1024]{1,0:T(8,128)(2,1)} %param.3) | copy-start | bytes 3145732
  255.4 339.0 %reduce-scatter.2.cloned.1.call-start = ((), (), s32[]{:S(2)}) async-start(), calls=%async_computation.5 | async-start | bytes 18874368 | tf_op jit(solution)/shard_map/reduce_scatter | solution.py:32
Sparse Core Ops, SparseCore 0:
  11.0 84.7 all-gather.3
  426.2 168.1 reduce-scatter.1
Sparse Core Ops, SparseCore 1:
  103.8 118.6 all-gather.5
  255.5 154.7 all-gather.7
where the time goes:
time: 605 us
  waiting for transfers between devices  519 us (86%)
  matrix products  46.4 us (8%)
  local copies, waits for them, and re-layouts  16.3 us (3%)
  between operations  15.5 us (3%)
    all_gather x1, waiting for transfers between devices, per_device(): grad_cols = lax.all_gather(weighted, 'row', axis=0, tiled=True)  155 us
    reduce_scatter x1, waiting for transfers between devices, per_device(): lax.psum_scatter(lax.dot_general(grad_cols, view_one, (((1,), (1,)), ((),...  152 us
    all_to_all x1, waiting for transfers between devices, per_device(): lax.all_to_all(wide_two, 'row', split_axis=1, concat_axis=0, tiled=True)  126 us
    all_gather x1, waiting for transfers between devices, per_device(): wide_two = lax.all_gather(view_two, 'col', axis=1, tiled=True)  85.4 us
    dot_general x1, matrix products, per_device(): lax.dot_general(regrouped, lax.all_gather(view_one, 'row', axis=0, tiled=...  15.8 us
    dot_general x1, matrix products, per_device(): lax.dot_general(grad_cols, view_one, (((1,), (1,)), ((), ())), preferred_...  15.8 us
    dot_general x1, matrix products, per_device(): jnp.dot(wide_two, grad_cols, preferred_element_type=jnp.float32)  14.8 us
  transfers between devices with their start and end apart: 5, of which 4 were waited for; matrix products, arithmetic and copies ran while one was open for 5% of the time, Pallas kernels for 0%

commit v1 on v0

--- a/solution.py
+++ b/solution.py
@@ -25,7 +25,12 @@
     )
     identity = jnp.where(row_ids == col_ids, 1.0, 0.0).astype(jnp.float32)
     weighted = (pair_weights.astype(jnp.float32) * (correlation - identity)).astype(jnp.bfloat16)
-    grad_cols = lax.all_gather(weighted, "row", axis=0, tiled=True)
+    ring = [weighted]
+    for hop in range(3):
+        ring.append(lax.ppermute(ring[-1], "row", [(dev, (dev + 1) % 4) for dev in range(4)]))
+    grad_cols = jnp.roll(
+        jnp.concatenate(ring[::-1], axis=0), (lax.axis_index("row") + 1) * ring[0].shape[0], axis=0
+    )
     first_grad = jnp.dot(wide_two, grad_cols, preferred_element_type=jnp.float32).astype(
         jnp.bfloat16
     )

time: 605 us -> 755 us (1.25)
  waiting for transfers between devices: 519 us -> 635 us
  local copies, waits for them, and re-layouts: 16.3 us -> 48.4 us
    ppermute x0 -> x3, waiting for transfers between devices: none -> 274 us  [per_device(): lax.ppermute(ring[-1], 'row', [(dev, (dev + 1) % 4) for dev in range(4)])]
    all_gather x1 -> x0, waiting for transfers between devices: 155 us -> none  [per_device(): grad_cols = lax.all_gather(weighted, 'row', axis=0, tiled=True)]
    unnamed x5 -> x20, local copies, waits for them, and re-layouts: 4.91 us -> 34.6 us
  transfers between devices with their start and end apart: 5 -> 7, of which waited for: 4 -> 6; matrix products, arithmetic and copies ran while one was open for 5% -> 4% of each run, Pallas kernels for 0% -> 0%
where the time goes in v1:
time: 755 us; the launch traced here: 754 us
  waiting for transfers between devices  635 us (84%)
  local copies, waits for them, and re-layouts  48.4 us (6%)
  matrix products  45.8 us (6%)
  between operations  15.6 us (2%)
  starting transfers between devices  7.69 us (1%)
    ppermute x3, waiting for transfers between devices, per_device(): lax.ppermute(ring[-1], 'row', [(dev, (dev + 1) % 4) for dev in range(4)])  274 us
    reduce_scatter x1, waiting for transfers between devices, per_device(): lax.psum_scatter(lax.dot_general(grad_cols, view_one, (((1,), (1,)), ((),...  149 us
    all_to_all x1, waiting for transfers between devices, per_device(): lax.all_to_all(wide_two, 'row', split_axis=1, concat_axis=0, tiled=True)  126 us
    all_gather x1, waiting for transfers between devices, per_device(): wide_two = lax.all_gather(view_two, 'col', axis=1, tiled=True)  85.4 us
    unnamed x20, local copies, waits for them, and re-layouts  34.6 us
    dot_general x1, matrix products, per_device(): lax.dot_general(grad_cols, view_one, (((1,), (1,)), ((), ())), preferred_...  15.8 us
    dot_general x1, matrix products, per_device(): jnp.dot(wide_two, grad_cols, preferred_element_type=jnp.float32)  15.6 us
  transfers between devices with their start and end apart: 7, of which 6 were waited for; matrix products, arithmetic and copies ran while one was open for 4% of the time, Pallas kernels for 0%

profile of v1, /device:TPU:0, one launch (start us, length us, event | category | flops | bytes accessed | tf_op | source)
XLA Modules:
  0.0 754.3 jit_solution(15340180576514604440)
XLA Ops:
  8.0 0.0 all-gather.3.cloned.1.call-start
  8.0 2.3 copy.9
  10.3 0.0 all-gather.3.cloned.1.call-update
  10.3 85.4 %all-gather.3.cloned.1.call-done = bf16[512,8192]{0,1:T(8,128)(2,1)} async-done(((bf16[512,1024]{0,1:T(8,128)(2,1)}), bf16[512,8192]{0,1:T(8,128)(2,1)}) %all-gather.3.cloned.1.call-update) | async-done | bytes 8388624 | tf_op jit(solution)/shard_map/all_gather | solution.py:8
  95.8 5.6 all-to-all-start
  101.4 0.0 all-gather.5.cloned.1.call-start
  101.5 0.5 all-gather.5.cloned.1.call-update
  102.0 0.0 reduce-scatter.2.cloned.1.call-start
  102.1 126.1 %all-to-all-done = bf16[512,4,2048]{0,2,1:T(8,128)(2,1)} async-done(((bf16[512,4,2048]{0,2,1:T(8,128)(2,1)}), bf16[512,4,2048]{0,2,1:T(8,128)(2,1)}, u32[]{:S(2)}, u32[]{:S(2)}) %all-to-all-start) | async-done | bytes 8388640 | tf_op jit(solution)/shard_map/all_to_all | solution.py:12
  228.1 11.4 %copy.10 = bf16[4,512,2048]{2,1,0:T(8,128)(2,1)} copy(bf16[4,512,2048]{1,2,0:T(8,128)(2,1)} %bitcast.1) | data formatting | bytes 16777216 | tf_op jit(solution)/shard_map/all_to_all | solution.py:12
  239.6 14.4 %multiply_convert_fusion = bf16[2048,1024]{1,0:T(8,128)(2,1)S(1)} fusion(bf16[2048,1024]{1,0:T(8,128)(2,1)} %param.5, bf16[2048,2048]{1,0:T(8,128)(2,1)} %bitcast.12, bf16[2048,1024]{1,0:T(8,128)(2,1)} %all-gather.5.cloned.1.call-done, s32[1024]{0:T(1024)S(1)} %iota_add_fusion.1, s32[2048]{0:T(1024)S(1)} %iota_add_fusion), kind=kOutput, calls=%fused_computation.4 | convolution fusion | flops 8604614656 | bytes 20983808 | tf_op jit(solution)/shard_map/dot_general | solution.py:13
  254.0 1.9 copy-done
  255.9 1.4 collective-permute-start
  257.3 91.3 %collective-permute-done = bf16[2048,1024]{1,0:T(8,128)(2,1)S(1)} collective-permute-done((bf16[2048,1024]{1,0:T(8,128)(2,1)S(1)}, bf16[2048,1024]{1,0:T(8,128)(2,1)S(1)}, u32[]{:S(2)}, u32[]{:S(2)}) %collective-permute-start) | collective-permute-done | bytes 4194336 | tf_op jit(solution)/shard_map/ppermute | solution.py:30
  348.7 1.9 copy-done.2
  350.6 0.5 collective-permute-start.1
  351.2 91.5 %collective-permute-done.1 = bf16[2048,1024]{1,0:T(8,128)(2,1)} collective-permute-done((bf16[2048,1024]{1,0:T(8,128)(2,1)S(1)}, bf16[2048,1024]{1,0:T(8,128)(2,1)}, u32[]{:S(2)}, u32[]{:S(2)}) %collective-permute-start.1) | collective-permute-done | bytes 4194336 | tf_op jit(solution)/shard_map/ppermute | solution.py:30
  442.6 91.3 %collective-permute-done.2 = bf16[2048,1024]{1,0:T(8,128)(2,1)} collective-permute-done((bf16[2048,1024]{1,0:T(8,128)(2,1)}, bf16[2048,1024]{1,0:T(8,128)(2,1)}, u32[]{:S(2)}, u32[]{:S(2)}) %collective-permute-start.2) | collective-permute-done | bytes 4194336 | tf_op jit(solution)/shard_map/ppermute | solution.py:30
  534.0 4.6 constant_dynamic-update-slice_fusion.7
  538.6 4.8 constant_dynamic-update-slice_fusion.6
  543.4 2.4 constant_dynamic-update-slice_fusion.5
  545.8 2.4 constant_dynamic-update-slice_fusion.4
  548.2 4.6 constant_dynamic-update-slice_fusion.3
  552.7 4.6 constant_dynamic-update-slice_fusion.2
  557.4 2.4 constant_dynamic-update-slice_fusion.1
  559.8 2.4 constant_dynamic-update-slice_fusion
  562.2 15.8 %fusion = f32[8192,512]{1,0:T(8,128)} fusion(bf16[512,1024]{1,0:T(8,128)(2,1)S(1)} %copy-done.4, bf16[16384,1024]{1,0:T(8,128)(2,1)} %constant_dynamic-update-slice_fusion, s32[]{:T(128)S(6)} %select_n.19), kind=kOutput, calls=%fused_computation | convolution fusion | flops 8589934592 | bytes 34603012 | tf_op jit(solution)/shard_map/dot_general | solution.py:38
  578.0 15.6 %fusion.7 = bf16[512,1024]{0,1:T(8,128)(2,1)S(1)} fusion(bf16[512,8192]{0,1:T(8,128)(2,1)} %all-gather.3.cloned.1.call-done, bf16[16384,1024]{1,0:T(8,128)(2,1)} %constant_dynamic-update-slice_fusion, s32[]{:T(128)S(6)} %select_n.19), kind=kOutput, calls=%fused_computation.6 | convolution fusion | flops 8590458880 | bytes 26214404 | tf_op jit(solution)/shard_map/dot_general | solution.py:34
  593.6 1.3 copy.11
  594.9 148.9 %reduce-scatter.2.cloned.1.call-done = f32[1024,512]{1,0:T(8,128)} async-done(((f32[8192,512]{1,0:T(8,128)}), f32[1024,512]{1,0:T(8,128)}) %reduce-scatter.2.cloned.1.call-update) | async-done | bytes 2097168 | tf_op jit(solution)/shard_map/reduce_scatter | solution.py:37
  743.9 1.7 convert_bitcast_fusion
  745.6 1.3 copy.12
  (13 shorter events, 0.0 us)
Async XLA Ops:
  8.0 87.8 %all-gather.3.cloned.1.call-start = ((), (), s32[]{:S(2)}) async-start(), calls=%async_computation.2 | async-start | bytes 9437184 | tf_op jit(solution)/shard_map/all_gather | solution.py:8
  95.8 132.4 %all-to-all-start = ((bf16[512,4,2048]{0,2,1:T(8,128)(2,1)}), bf16[512,4,2048]{0,2,1:T(8,128)(2,1)}, u32[]{:S(2)}, u32[]{:S(2)}) async-start(bf16[512,4,2048]{0,2,1:T(8,128)(2,1)} %bitcast.11), calls=%async_computation | async-start | bytes 16777216 | tf_op jit(solution)/shard_map/all_to_all | solution.py:12
  101.4 138.2 %all-gather.5.cloned.1.call-start = ((), (), s32[]{:S(2)}) async-start(), calls=%async_computation.3 | async-start | bytes 5242880 | tf_op jit(solution)/shard_map/all_gather | solution.py:15
  102.0 641.9 %reduce-scatter.2.cloned.1.call-start = ((), (), s32[]{:S(2)}) async-start(), calls=%async_computation.4 | async-start | bytes 18874368 | tf_op jit(solution)/shard_map/reduce_scatter | solution.py:37
  254.0 1.9 copy-start
  255.9 92.8 %collective-permute-start = (bf16[2048,1024]{1,0:T(8,128)(2,1)S(1)}, bf16[2048,1024]{1,0:T(8,128)(2,1)S(1)}, u32[]{:S(2)}, u32[]{:S(2)}) collective-permute-start(bf16[2048,1024]{1,0:T(8,128)(2,1)S(1)} %multiply_convert_fusion), channel_id=1, source_target_pairs={{0,8},{8,16},{16,24},{24,0},{1,9},{9,17},{17,25},{25,1},{2,10},{10... | collective-permute-start | bytes 12582920 | tf_op jit(solution)/shard_map/ppermute | solution.py:30
  348.7 1.9 copy-start.2
  350.6 92.0 %collective-permute-start.1 = (bf16[2048,1024]{1,0:T(8,128)(2,1)S(1)}, bf16[2048,1024]{1,0:T(8,128)(2,1)}, u32[]{:S(2)}, u32[]{:S(2)}) collective-permute-start(bf16[2048,1024]{1,0:T(8,128)(2,1)S(1)} %collective-permute-done), channel_id=1, source_target_pairs={{0,8},{8,16},{16,24},{24,0},{1,9},{9,17},{17,25},{25,1},{2,10},{10... | collective-permute-start | bytes 12582920 | tf_op jit(solution)/shard_map/ppermute | solution.py:30
  442.6 91.4 %collective-permute-start.2 = (bf16[2048,1024]{1,0:T(8,128)(2,1)}, bf16[2048,1024]{1,0:T(8,128)(2,1)}, u32[]{:S(2)}, u32[]{:S(2)}) collective-permute-start(bf16[2048,1024]{1,0:T(8,128)(2,1)} %collective-permute-done.1), channel_id=1, source_target_pairs={{0,8},{8,16},{16,24},{24,0},{1,9},{9,17},{17,25},{25,1},{2,10},{10... | collective-permute-start | bytes 12582920 | tf_op jit(solution)/shard_map/ppermute | solution.py:30
  442.6 100.7 %copy-start.3 = (bf16[2048,1024]{1,0:T(8,128)(2,1)S(1)}, bf16[2048,1024]{1,0:T(8,128)(2,1)}, u32[]{:S(2)}) copy-start(bf16[2048,1024]{1,0:T(8,128)(2,1)} %copy-done.2) | copy-start | bytes 12582916
  538.6 7.2 copy-start.1
  557.4 4.8 copy-start.4
Sparse Core Ops, SparseCore 0:
  11.0 84.7 all-gather.2
  578.1 165.7 reduce-scatter.1
Sparse Core Ops, SparseCore 1:
  103.7 118.6 all-gather.4
